TPU v7x, 32 devices: a whole 2x2x4 slice. The times are simulated.
32 devices in a mesh: row: 4 (over y, x), col: 8 (over z, core).
Axes of the slice: x: 2, y: 2, z: 4, core: 2. Of those that a mesh axis runs over, the one named last changes fastest.
Arguments:
- activations: bfloat16 [1024, 9216], P('col', 'row'), may hold values from -64 to 64
- output_grads: bfloat16 [1024, 73728], P('row', 'col'), may hold values from -16 to 16
- weight: bfloat16 [9216, 73728], P('row', 'col'), may hold values from -1 to 1
- row_moment: float32 [9216], P('row'), may hold values from 0.01 to 0.3
- col_moment: float32 [73728], P('col'), may hold values from 0.01 to 0.3
Outputs:
- new_weight: bfloat16 [9216, 73728], P('row', 'col')
- new_row: float32 [9216], P('row')
- new_col: float32 [73728], P('col')
All inputs are finite; a program needn't handle non-finite values.
Results may differ from a plain program's by a relative error of at most 0.0004.
Values may be sent and summed in bfloat16 or wider, within the bound.
A program may use at most 256 MiB of HBM per device.

v0:
```python
import functools

import jax
import jax.numpy as jnp
from jax import lax
from jax.experimental import pallas as pl
from jax.experimental.pallas import tpu as pltpu
from jax.sharding import PartitionSpec as P

ADDED_SQUARE = 1e-30
DECAY_RATE = 0.8
CLIP_LIMIT = 1.0
STEP_SIZE = 0.1
MEAN_OFFSET = 1e-06

MESH = pl.DeviceIdType.MESH
WIDTH = 512
BLOCKS = 1
KEEP = 2
DOTS = 1
PIECES = 3
AHEAD = 3
LAG = 2
SLOTS = LAG + 1
ACTS_FORWARD = 4
ACTS_READY = 6


def lane_sum(x):
    out = x[:, :128]
    for k in range(1, x.shape[1] // 128):
        out = out + x[:, k * 128 : (k + 1) * 128]
    return out


def sublane_sum(x):
    return jnp.sum(x.reshape(x.shape[0] // 8, 8, x.shape[1]), axis=0)


def gather_kernel(
    rows, cols,
    acts_ref, og_ref, w_ref, rm_ref, cm_ref,
    og_out, at_out, g_out, nr_out, nc_out, rs_out, cs_out,
    og_all, acts_all, acts_t, grad, wbuf, rowacc, sacc, wacc, colx, rowx, scb, scc,
    load_sem, og_sem, acts_sem, sib_sem, col_sem, row_sem, scb_sem, scc_sem, w_sem, out_sem, g_sem, misc_sem,
):
    n, tokens, width = og_all.shape
    tile_rows = acts_t.shape[0]
    tall = grad.shape[2]
    kept = tall // KEEP
    sub = tile_rows // PIECES
    blocks = tile_rows // tall
    share = tokens // rows
    half = share // 2
    wrows = tile_rows // n
    total_rows = tile_rows * rows
    total_cols = n * width * cols
    entries = float(total_rows * total_cols)
    r, c = lax.axis_index("row"), lax.axis_index("col")
    rx = r + 1 - 2 * lax.rem(r, 2)
    ry = lax.rem(r + 2, 4)
    rd = lax.rem(rx + 2, 4)
    sib = c + 1 - 2 * lax.rem(c, 2)

    def region(owner, start, size):
        return pl.ds(pl.multiple_of(owner * share + start, half), size)

    def load(j):
        return pltpu.make_async_copy(
            og_ref.at[:, pl.ds(pl.multiple_of(j * width, width), width)],
            og_all.at[j, region(r, 0, share), :], load_sem.at[j])

    def og_copy(j, kind, owner, start, size, to):
        ref = og_all.at[j, region(owner, start, size), :]
        return pltpu.make_async_remote_copy(
            src_ref=ref, dst_ref=ref, send_sem=og_sem.at[0, kind, j], recv_sem=og_sem.at[1, kind, j],
            device_id={"row": to}, device_id_type=MESH)

    def own_x(j):
        return og_copy(j, 0, r, 0, share, rx)

    def own_y(j):
        return og_copy(j, 1, r, 0, share, ry)

    def fwd_y(j):
        return og_copy(j, 2, rx, 0, half, ry)

    def fwd_x(j):
        return og_copy(j, 3, ry, half, half, rx)

    def acts_copy(d):
        to = lax.rem(c + 2 * d, cols)
        return pltpu.make_async_remote_copy(
            src_ref=acts_all.at[c], dst_ref=acts_all.at[c], send_sem=acts_sem.at[0, d], recv_sem=acts_sem.at[1, d],
            device_id={"col": to}, device_id_type=MESH)

    def sib_copy(d):
        at = lax.rem(c + cols - 2 * d, cols)
        return pltpu.make_async_remote_copy(
            src_ref=acts_all.at[at], dst_ref=acts_all.at[at], send_sem=sib_sem.at[0, d], recv_sem=sib_sem.at[1, d],
            device_id={"col": sib}, device_id_type=MESH)

    def col_copy(j, d):
        return pltpu.make_async_remote_copy(
            src_ref=colx.at[r, j], dst_ref=colx.at[r, j], send_sem=col_sem.at[0, d, j], recv_sem=col_sem.at[1, d, j],
            device_id={"row": lax.rem(r + d, rows)}, device_id_type=MESH)

    def row_copy(d):
        return pltpu.make_async_remote_copy(
            src_ref=rowx.at[c], dst_ref=rowx.at[c], send_sem=row_sem.at[0, d], recv_sem=row_sem.at[1, d],
            device_id={"col": lax.rem(c + d, cols)}, device_id_type=MESH)

    def scb_copy(d):
        return pltpu.make_async_remote_copy(
            src_ref=scb.at[c], dst_ref=scb.at[c], send_sem=scb_sem.at[0, d], recv_sem=scb_sem.at[1, d],
            device_id={"col": lax.rem(c + d, cols)}, device_id_type=MESH)

    def scc_copy(d):
        return pltpu.make_async_remote_copy(
            src_ref=scc.at[r], dst_ref=scc.at[r], send_sem=scc_sem.at[0, d], recv_sem=scc_sem.at[1, d],
            device_id={"row": lax.rem(r + d, rows)}, device_id_type=MESH)

    def w_copy(j):
        return pltpu.make_async_copy(
            w_ref.at[pl.ds(pl.multiple_of(j * wrows, wrows), wrows), :], wbuf.at[lax.rem(j, 2)], w_sem.at[lax.rem(j, 2)])

    def og_store(j):
        return pltpu.make_async_copy(og_all.at[j], og_out.at[j], out_sem.at[j])

    def g_store(j):
        s = lax.rem(j, SLOTS)
        return pltpu.make_async_copy(grad.at[s, :, pl.ds(tall - kept, kept), :], g_out.at[j], g_sem.at[s])

    acts_load = pltpu.make_async_copy(acts_ref, acts_all.at[c], misc_sem.at[0])
    acts_store = pltpu.make_async_copy(acts_t, at_out, misc_sem.at[1])

    acts_load.start()

    @pl.loop(0, n)
    def _(j):
        load(j).start()

    w_copy(0).start()
    w_copy(1).start()

    barrier = pltpu.get_barrier_semaphore()
    for d in range(1, rows):
        pl.semaphore_signal(barrier, inc=1, device_id={"row": lax.rem(r + d, rows)}, device_id_type=MESH)
    for d in range(1, cols):
        pl.semaphore_signal(barrier, inc=1, device_id={"col": lax.rem(c + d, cols)}, device_id_type=MESH)
    rowacc[...] = jnp.zeros_like(rowacc)
    sacc[...] = jnp.zeros_like(sacc)
    wacc[...] = jnp.zeros_like(wacc)
    pl.semaphore_wait(barrier, rows + cols - 2)

    def send_own(j):
        load(j).wait()
        own_x(j).start()
        own_y(j).start()

    for j in range(AHEAD):
        send_own(j)
    acts_load.wait()
    for d in range(1, cols // 2):
        acts_copy(d).start()
    sib_copy(0).start()

    def exchange(j):
        own_x(j).wait_recv()
        fwd_y(j).start()
        own_y(j).wait_recv()
        fwd_x(j).start()

        @pl.when(j + AHEAD < n)
        def _():
            send_own(j + AHEAD)

    def weigh(j):
        w_copy(j).wait()
        s = lax.rem(j, 2)
        wide = 1024

        @pl.loop(0, wbuf.shape[2] // wide)
        def _(k):
            x = wbuf[s, :, pl.ds(pl.multiple_of(k * wide, wide), wide)].astype(jnp.float32)
            wacc[...] += sublane_sum(x * x)

        @pl.when(j + 2 < n)
        def _():
            w_copy(j + 2).start()

    def stats(k):
        for d in range(1, rows):
            col_copy(k, d).wait_recv()
        total = colx[0, k]
        for q in range(1, rows):
            total = total + colx[q, k]
        factor = DECAY_RATE * cm_ref[k] + (1.0 - DECAY_RATE) * total / total_rows
        nc_out[k] = factor
        cs_out[k] = lax.rsqrt(factor)
        weight = 1.0 / factor
        s = lax.rem(k, SLOTS)
        for b in range(blocks):
            @pl.loop(0, tall // sub)
            def _(i):
                at = pl.ds(pl.multiple_of(i * sub, sub), sub)
                g = grad[s, b, at, :]
                to = pl.ds(pl.multiple_of(b * tall + i * sub, sub), sub)
                sacc[to, :] += lane_sum(g * g * weight)

    def compute(k):
        fwd_y(k).wait_recv()
        fwd_x(k).wait_recv()
        og_store(k).start()
        s = lax.rem(k, SLOTS)

        @pl.when(k >= SLOTS)
        def _():
            g_store(k - SLOTS).wait()

        right = og_all.at[k]
        column = jnp.zeros((8, width), jnp.float32)
        for b in range(blocks):
            def step(i, column):
                to = pl.ds(pl.multiple_of(b * tall + i * sub, sub), sub)
                g = jnp.dot(acts_t[to, :], right[...], preferred_element_type=jnp.float32)
                grad[s, b, pl.ds(pl.multiple_of(i * sub, sub), sub), :] = g
                squared = g * g + ADDED_SQUARE
                rowacc[to, :] += lane_sum(squared)
                return column + sublane_sum(squared)
            column = lax.fori_loop(0, tall // sub, step, column)
        colx[r, k] = jnp.sum(column, axis=0, keepdims=True)
        for d in range(1, rows):
            col_copy(k, d).start()
        g_store(k).start()

        @pl.when(k >= LAG)
        def _():
            stats(k - LAG)

    def reach(j):
        return jnp.minimum(j, 2 * (j - ACTS_READY + 1))

    @pl.loop(0, ACTS_FORWARD)
    def _(j):
        exchange(j)
        weigh(j)

    for d in range(1, cols // 2):
        acts_copy(d).wait_recv()
        sib_copy(d).start()

    @pl.loop(ACTS_FORWARD, ACTS_READY)
    def _(j):
        exchange(j)
        weigh(j)

    for d in range(cols // 2):
        sib_copy(d).wait_recv()
    part = acts_all.shape[1]
    for q in range(cols):
        acts_t[:, q * part : (q + 1) * part] = acts_all[q].T
    acts_store.start()

    @pl.loop(ACTS_READY, n)
    def _(j):
        exchange(j)
        weigh(j)

        @pl.loop(reach(j - 1), reach(j))
        def _(k):
            compute(k)

    @pl.loop(n - 1, n)
    def _(k):
        compute(k)

    rowx[c] = jnp.sum(rowacc[...].T, axis=0, keepdims=True)
    for d in range(1, cols):
        row_copy(d).start()

    @pl.loop(n - LAG, n)
    def _(k):
        stats(k)

    ratio_rows = jnp.sum(sacc[...].T, axis=0, keepdims=True)
    for d in range(1, cols):
        row_copy(d).wait_recv()
    row_total = rowx[0]
    for q in range(1, cols):
        row_total = row_total + rowx[q]
    new_row = DECAY_RATE * rm_ref[...] + (1.0 - DECAY_RATE) * row_total / total_cols
    nr_out[...] = new_row

    def spread(x):
        return jnp.broadcast_to(jnp.sum(x, axis=1, keepdims=True), (1, 128))

    scb[c, 0:1, :] = spread(ratio_rows / new_row)
    scb[c, 1:2, :] = spread(jnp.sum(wacc[...], axis=0, keepdims=True))
    for d in range(1, cols):
        scb_copy(d).start()
    row_sum = spread(new_row)
    for d in range(1, cols):
        scb_copy(d).wait_recv()
    both = scb[0]
    for q in range(1, cols):
        both = both + scb[q]
    scc[r, 0:2, :] = both[0:2, :]
    scc[r, 2:3, :] = row_sum
    for d in range(1, rows):
        scc_copy(d).start()
    root = lax.rsqrt(new_row)
    for d in range(1, rows):
        scc_copy(d).wait_recv()
    every = scc[0]
    for q in range(1, rows):
        every = every + scc[q]
    row_mean = every[2:3, :] / total_rows
    rms_update = jnp.sqrt(row_mean * (every[0:1, :] / entries))
    clip_factor = jnp.maximum(1.0, rms_update / CLIP_LIMIT)
    step_scale = STEP_SIZE * jnp.sqrt(every[1:2, :] / entries + MEAN_OFFSET)
    scale = step_scale / clip_factor * jnp.sqrt(row_mean)
    rs_out[...] = jnp.broadcast_to(root, (128, tile_rows)).T * scale

    @pl.loop(0, n)
    def _(j):
        own_x(j).wait_send()
        own_y(j).wait_send()
        fwd_y(j).wait_send()
        fwd_x(j).wait_send()
        og_store(j).wait()
        for d in range(1, rows):
            col_copy(j, d).wait_send()

    @pl.loop(n - SLOTS, n)
    def _(j):
        g_store(j).wait()

    acts_store.wait()
    for d in range(1, cols // 2):
        acts_copy(d).wait_send()
    for d in range(cols // 2):
        sib_copy(d).wait_send()
    for d in range(1, cols):
        row_copy(d).wait_send()
        scb_copy(d).wait_send()
    for d in range(1, rows):
        scc_copy(d).wait_send()


def update_kernel(at_ref, og_ref, w_ref, g_ref, rs_ref, cs_ref, out_ref):
    i = pl.program_id(1)
    tall, width = w_ref.shape
    j = pl.program_id(0)
    cs = cs_ref[j]
    kept = tall // KEEP
    sub = (tall - kept) // DOTS

    def finish(g, at):
        rs = rs_ref[pl.ds(pl.multiple_of(i * tall + at.start, 16), at.size), :]
        wide = jnp.concatenate([rs] * (width // 128), axis=1)
        out_ref[at, :] = (w_ref[at, :].astype(jnp.float32) - g * wide * cs).astype(out_ref.dtype)

    finish(g_ref[0, 0], pl.ds(tall - kept, kept))
    for k in range(DOTS):
        left = at_ref[pl.ds(pl.multiple_of(i * tall + k * sub, 16), sub), :]
        g = jnp.dot(left, og_ref[0], preferred_element_type=jnp.float32)
        finish(g, pl.ds(k * sub, sub))


def with_kernels(rows, cols, activations, output_grads, weight, row_moment, col_moment):
    tile_rows, tile_cols = weight.shape
    part = activations.shape[0]
    tokens = part * cols
    n, width = tile_cols // WIDTH, WIDTH
    blocks = BLOCKS
    tall = tile_rows // blocks
    kept = tall // KEEP
    f32, bf16 = jnp.float32, jnp.bfloat16
    any_space = pl.BlockSpec(memory_space=pl.ANY)
    vmem = pl.BlockSpec(memory_space=pltpu.VMEM)
    dma = pltpu.SemaphoreType.DMA
    flops = 2 * tile_rows * tile_cols * tokens
    og_all, acts_t, grads, new_row, new_col, rs, cs = pl.pallas_call(
        functools.partial(gather_kernel, rows, cols),
        out_shape=(
            jax.ShapeDtypeStruct((n, tokens, width), bf16),
            jax.ShapeDtypeStruct((tile_rows, tokens), bf16),
            jax.ShapeDtypeStruct((n, blocks, kept, width), f32),
            jax.ShapeDtypeStruct((1, tile_rows), f32),
            jax.ShapeDtypeStruct((n, 1, width), f32),
            jax.ShapeDtypeStruct((tile_rows, 128), f32),
            jax.ShapeDtypeStruct((n, 1, width), f32),
        ),
        in_specs=[any_space, any_space, any_space, vmem, vmem],
        out_specs=(any_space, any_space, any_space, vmem, vmem, vmem, vmem),
        scratch_shapes=[
            pltpu.VMEM((n, tokens, width), bf16),
            pltpu.VMEM((cols, part, tile_rows), bf16),
            pltpu.VMEM((tile_rows, tokens), bf16),
            pltpu.VMEM((SLOTS, blocks, tall, width), f32),
            pltpu.VMEM((2, tile_rows // n, tile_cols), bf16),
            pltpu.VMEM((tile_rows, 128), f32),
            pltpu.VMEM((tile_rows, 128), f32),
            pltpu.VMEM((8, 1024), f32),
            pltpu.VMEM((rows, n, 1, width), f32),
            pltpu.VMEM((cols, 1, tile_rows), f32),
            pltpu.VMEM((cols, 2, 128), f32),
            pltpu.VMEM((rows, 3, 128), f32),
            dma((n,)), dma((2, 4, n)), dma((2, cols // 2)), dma((2, cols // 2)), dma((2, rows, n)),
            dma((2, cols)), dma((2, cols)), dma((2, rows)), dma((2,)), dma((n,)), dma((SLOTS,)), dma((2,)),
        ],
        compiler_params=pltpu.CompilerParams(
            collective_id=0, has_side_effects=True, vmem_limit_bytes=62 * 1024 * 1024),
        cost_estimate=pl.CostEstimate(flops=flops, bytes_accessed=2 * weight.size, transcendentals=0),
        name="gather_stats",
    )(activations, output_grads, weight, row_moment.reshape(1, tile_rows), col_moment.reshape(n, 1, width))
    new_weight = pl.pallas_call(
        update_kernel,
        grid=(n, blocks),
        out_shape=jax.ShapeDtypeStruct((tile_rows, tile_cols), bf16),
        in_specs=[
            pl.BlockSpec((tile_rows, tokens), lambda j, i: (0, 0)),
            pl.BlockSpec((1, tokens, width), lambda j, i: (j, 0, 0)),
            pl.BlockSpec((tall, width), lambda j, i: (i, j)),
            pl.BlockSpec((1, 1, kept, width), lambda j, i: (j, i, 0, 0)),
            vmem,
            vmem,
        ],
        out_specs=pl.BlockSpec((tall, width), lambda j, i: (i, j)),
        compiler_params=pltpu.CompilerParams(
            dimension_semantics=("arbitrary", "arbitrary"), vmem_limit_bytes=48 * 1024 * 1024),
        cost_estimate=pl.CostEstimate(flops=flops, bytes_accessed=4 * weight.size, transcendentals=0),
        name="update_weight",
    )(acts_t, og_all, weight, grads, rs, cs)
    return new_weight, new_row.reshape(tile_rows), new_col.reshape(tile_cols)


def plain(activations, output_grads, weight, row_moment, col_moment):
    tile_rows, tile_cols = weight.shape
    total_rows = tile_rows * lax.axis_size("row")
    total_cols = tile_cols * lax.axis_size("col")
    entries = float(total_rows * total_cols)
    weight_wide = weight.astype(jnp.float32)
    weight_local = jnp.sum(weight_wide * weight_wide)
    weight_total = lax.psum(weight_local, ("row", "col"))
    contract = (((0,), (0,)), ((), ()))
    acts_all = lax.all_gather(activations, "col", axis=0, tiled=True)
    gradient = lax.dot_general(
        acts_all,
        lax.all_gather(output_grads, "row", axis=0, tiled=True),
        contract,
        preferred_element_type=jnp.float32,
    )
    squared = gradient * gradient
    row_part = jnp.sum(squared + ADDED_SQUARE, axis=1)
    col_part = jnp.sum(squared + ADDED_SQUARE, axis=0)
    row_total = lax.psum(row_part, "col")
    col_total = lax.psum(col_part, "row")
    new_row = DECAY_RATE * row_moment + (1.0 - DECAY_RATE) * row_total / total_cols
    new_col = DECAY_RATE * col_moment + (1.0 - DECAY_RATE) * col_total / total_rows
    inverse = lax.rsqrt(new_row[:, None] * new_col[None, :])
    ratio_local = jnp.sum(squared * inverse * inverse)
    leader = (lax.axis_index("col") == 0).astype(jnp.float32)
    row_local = leader * jnp.sum(new_row)
    row_sum, ratio_sum = lax.psum((row_local, ratio_local), ("row", "col"))
    row_mean = row_sum / total_rows
    rms_update = jnp.sqrt(row_mean * ratio_sum / entries)
    clip_factor = jnp.maximum(1.0, rms_update / CLIP_LIMIT)
    step_scale = STEP_SIZE * jnp.sqrt(weight_total / entries + MEAN_OFFSET)
    update = gradient * inverse * jnp.sqrt(row_mean)
    new_weight = (weight_wide - step_scale / clip_factor * update).astype(jnp.bfloat16)
    return (new_weight, new_row, new_col)


def on_device(rows, cols, activations, output_grads, weight, row_moment, col_moment):
    tile_rows, tile_cols = weight.shape
    chunks = tile_cols // WIDTH
    fits = (
        rows == 4 and cols % 2 == 0 and cols > 2
        and tile_rows % (64 * BLOCKS * KEEP * DOTS) == 0 and tile_rows % (16 * BLOCKS * PIECES) == 0 and tile_cols % 1024 == 0
        and chunks > ACTS_READY + SLOTS and tile_rows % (16 * chunks) == 0
        and output_grads.shape[0] % 32 == 0 and activations.shape[0] % 128 == 0
    )
    args = (activations, output_grads, weight, row_moment, col_moment)
    return with_kernels(rows, cols, *args) if fits else plain(*args)


def solution(mesh):
    return jax.shard_map(
        functools.partial(on_device, mesh.shape["row"], mesh.shape["col"]),
        mesh=mesh,
        in_specs=(P("col", "row"), P("row", "col"), P("row", "col"), P("row"), P("col")),
        out_specs=(P("row", "col"), P("row"), P("col")),
        check_vma=False,
    )
```

profile of v0, /device:TPU:0, one launch (start us, length us, event | category | flops | bytes accessed | tf_op | source)
XLA Modules:
  0.0 254.2 jit_solution(7034388351575643934)
XLA Ops:
  0.6 1.3 reshape.18.rm_ref
  1.9 185.0 %gather_stats.1 = (bf16[18,1024,512]{2,1,0:T(8,128)(2,1)}, bf16[2304,1024]{1,0:T(8,128)(2,1)}, f32[18,1,1152,512]{3,2,1,0:T(8,128)}, f32[1,2304]{1,0:T(1,128)}, ...) custom-call(bf16[128,2304]{1,0:T(8,128)(2,1)} %acts_ref.1, bf16[256,9216]{1,0:T(8,128)(2,1)} %og_ref.1, ...), custom_call_target="tpu_custom_call" | custom-call | flops 43486543872 | bytes 42467328 | tf_op jit(solution)/shard_map/gather_stats/pallas_call | solution.py:384
  186.9 0.0 copy-start
  187.0 2.3 copy-done
  189.3 0.0 copy-start.1
  189.3 1.3 copy-done.1
  190.6 0.0 copy-start.2
  190.6 0.8 copy-done.2
  191.3 0.0 copy-start.4
  191.3 0.0 copy-start.3
  191.3 61.6 %update_weight.1 = bf16[2304,9216]{1,0:T(8,128)(2,1)} custom-call(bf16[2304,1024]{1,0:T(8,128)(2,1)S(1)} %copy-done, bf16[18,1024,512]{2,1,0:T(8,128)(2,1)} %get-tuple-element.11.og_ref, bf16[2304,9216]{1,0:T(8,128)(2,1)} %w_ref.3, f32[18,1,1152,512]{3,2,1,0:T(8,128)} %get-tuple-element.12.g_ref, f32[2304,128]{1,0:T(8,128)S(1)} %copy-done.1, ...), custom_call_target="tpu_custom_call" | custom-call | flops 43486543872 | bytes 84934656 | tf_op jit(solution)/shard_map/update_weight/pallas_call | solution.py:418
  253.0 0.0 copy-done.4
  253.0 0.6 reduce
  253.6 0.0 copy-done.3
  253.6 0.6 copy.9
Async XLA Ops:
  186.9 2.3 copy-start
  189.3 1.3 copy-start.1
  190.6 0.8 copy-start.2
  191.3 61.6 %copy-start.4 = (f32[1,2304]{1,0:T(1,128)S(1)}, f32[1,2304]{1,0:T(1,128)}, u32[]{:S(2)}) copy-start(f32[1,2304]{1,0:T(1,128)} %get-tuple-element.15) | copy-start | bytes 27652
  191.3 62.3 %copy-start.3 = (f32[18,1,512]{2,1,0:T(1,128)S(1)}, f32[18,1,512]{2,1,0:T(1,128)}, u32[]{:S(2)}) copy-start(f32[18,1,512]{2,1,0:T(1,128)} %get-tuple-element.16) | copy-start | bytes 110596
where the time goes:
time: 255 us; the launch traced here: 254 us
  Pallas kernels  247 us (97%)
  local copies, waits for them, and re-layouts  6.31 us (2%)
    pallas_call x1, Pallas kernels, with_kernels(): pl.pallas_call(functools.partial(gather_kernel, rows, cols), out_shape=(j...  185 us
    pallas_call x1, Pallas kernels, with_kernels(): pl.pallas_call(update_kernel, grid=(n, blocks), out_shape=jax.ShapeDtypeS...  61.6 us

commit v1 on v0

--- a/solution.py
+++ b/solution.py
@@ -15,15 +15,25 @@
 
 MESH = pl.DeviceIdType.MESH
 WIDTH = 512
-BLOCKS = 1
-KEEP = 2
-DOTS = 1
 PIECES = 3
 AHEAD = 3
 LAG = 2
 SLOTS = LAG + 1
+FIXED = 2
+KEPT = FIXED + SLOTS
+PARTS = 4
+WEIGHINGS = 4
+W_RING = 3
+DOT_PARTS = 2
+SPLIT = 2
+RING = 5
+LOADS = 2
+OG_RING = LOADS + 1
+ROWS = 256
 ACTS_FORWARD = 4
 ACTS_READY = 6
+GATHER_VMEM = 23800 * 1024
+UPDATE_VMEM = 22500 * 1024
 
 
 def lane_sum(x):
@@ -37,22 +47,35 @@
     return jnp.sum(x.reshape(x.shape[0] // 8, 8, x.shape[1]), axis=0)
 
 
+def slot_of(k):
+    return jnp.where(k < FIXED, k, FIXED + lax.rem(k - FIXED + FIXED * SLOTS, SLOTS))
+
+
+def chunk_in(s, n):
+    base = n - SLOTS
+    return jnp.where(s < FIXED, s, base + lax.rem(s + SLOTS * n - base, SLOTS))
+
+
 def gather_kernel(
     rows, cols,
-    acts_ref, og_ref, w_ref, rm_ref, cm_ref,
-    og_out, at_out, g_out, nr_out, nc_out, rs_out, cs_out,
-    og_all, acts_all, acts_t, grad, wbuf, rowacc, sacc, wacc, colx, rowx, scb, scc,
-    load_sem, og_sem, acts_sem, sib_sem, col_sem, row_sem, scb_sem, scc_sem, w_sem, out_sem, g_sem, misc_sem,
+    acts_ref, og_ref, w_ref, rm_ref, cm_ref, *refs,
 ):
+    og_out, nr_out, nc_out, rs_out, cs_out, *refs = refs
+    acts_t, refs = refs[:PIECES], refs[PIECES:]
+    grad, refs = refs[: PIECES * PARTS], refs[PIECES * PARTS :]
+    og_all, wbuf, rowacc, wacc, colx, rowx, scb, scc, *sems = refs
+    load_sem, og_sem, acts_sem, sib_sem, col_sem, row_sem, scb_sem, scc_sem, w_sem, misc_sem, out_sem = sems
     n, tokens, width = og_all.shape
-    tile_rows = acts_t.shape[0]
-    tall = grad.shape[2]
-    kept = tall // KEEP
-    sub = tile_rows // PIECES
-    blocks = tile_rows // tall
+    sub = acts_t[0].shape[0]
+    tile_rows = sub * PIECES
+    thin = sub // PARTS
+    part = acts_ref.shape[0]
+    spans = -(-tile_rows // width)
+    shared = -(-spans // 2)
     share = tokens // rows
     half = share // 2
-    wrows = tile_rows // n
+    wrows = wbuf.shape[1]
+    sacc = rs_out
     total_rows = tile_rows * rows
     total_cols = n * width * cols
     entries = float(total_rows * total_cols)
@@ -88,17 +111,22 @@
     def fwd_x(j):
         return og_copy(j, 3, ry, half, half, rx)
 
-    def acts_copy(d):
+    def acts_part(i, q):
+        return acts_t[i].at[:, pl.ds(pl.multiple_of(q * part, part), part)]
+
+    def acts_copies(d):
         to = lax.rem(c + 2 * d, cols)
-        return pltpu.make_async_remote_copy(
-            src_ref=acts_all.at[c], dst_ref=acts_all.at[c], send_sem=acts_sem.at[0, d], recv_sem=acts_sem.at[1, d],
-            device_id={"col": to}, device_id_type=MESH)
-
-    def sib_copy(d):
+        return [pltpu.make_async_remote_copy(
+            src_ref=acts_part(i, c), dst_ref=acts_part(i, c),
+            send_sem=acts_sem.at[0, d, i], recv_sem=acts_sem.at[1, d, i],
+            device_id={"col": to}, device_id_type=MESH) for i in range(PIECES)]
+
+    def sib_copies(d):
         at = lax.rem(c + cols - 2 * d, cols)
-        return pltpu.make_async_remote_copy(
-            src_ref=acts_all.at[at], dst_ref=acts_all.at[at], send_sem=sib_sem.at[0, d], recv_sem=sib_sem.at[1, d],
-            device_id={"col": sib}, device_id_type=MESH)
+        return [pltpu.make_async_remote_copy(
+            src_ref=acts_part(i, at), dst_ref=acts_part(i, at),
+            send_sem=sib_sem.at[0, d, i], recv_sem=sib_sem.at[1, d, i],
+            device_id={"col": sib}, device_id_type=MESH) for i in range(PIECES)]
 
     def col_copy(j, d):
         return pltpu.make_async_remote_copy(
@@ -122,26 +150,29 @@
 
     def w_copy(j):
         return pltpu.make_async_copy(
-            w_ref.at[pl.ds(pl.multiple_of(j * wrows, wrows), wrows), :], wbuf.at[lax.rem(j, 2)], w_sem.at[lax.rem(j, 2)])
+            w_ref.at[pl.ds(pl.multiple_of(j * wrows, wrows), wrows), :], wbuf.at[lax.rem(j, W_RING)], w_sem.at[lax.rem(j, W_RING)])
 
     def og_store(j):
         return pltpu.make_async_copy(og_all.at[j], og_out.at[j], out_sem.at[j])
 
-    def g_store(j):
-        s = lax.rem(j, SLOTS)
-        return pltpu.make_async_copy(grad.at[s, :, pl.ds(tall - kept, kept), :], g_out.at[j], g_sem.at[s])
-
-    acts_load = pltpu.make_async_copy(acts_ref, acts_all.at[c], misc_sem.at[0])
-    acts_store = pltpu.make_async_copy(acts_t, at_out, misc_sem.at[1])
-
-    acts_load.start()
-
-    @pl.loop(0, n)
+    def acts_span(m):
+        return n - 1 - m // 2, pl.ds(pl.multiple_of(r * share + m % 2 * part, part), part), min(width, tile_rows - m * width)
+
+    def acts_load(m):
+        slab, at, lanes = acts_span(m)
+        return pltpu.make_async_copy(
+            acts_ref.at[:, pl.ds(m * width, lanes)], og_all.at[slab, at, pl.ds(0, lanes)], misc_sem.at[m])
+
+
+    for m in range(spans):
+        acts_load(m).start()
+
+    @pl.loop(0, n - shared)
     def _(j):
         load(j).start()
 
-    w_copy(0).start()
-    w_copy(1).start()
+    for j in range(W_RING):
+        w_copy(j).start()
 
     barrier = pltpu.get_barrier_semaphore()
     for d in range(1, rows):
@@ -151,6 +182,18 @@
     rowacc[...] = jnp.zeros_like(rowacc)
     sacc[...] = jnp.zeros_like(sacc)
     wacc[...] = jnp.zeros_like(wacc)
+    own = pl.ds(pl.multiple_of(c * part, part), part)
+    for m in range(spans):
+        acts_load(m).wait()
+        slab, at, lanes = acts_span(m)
+        for o in range(0, lanes, ROWS):
+            i, low = divmod(m * width + o, sub)
+            acts_t[i][low : low + ROWS, own] = og_all[slab, at, o : o + ROWS].T
+
+    @pl.loop(n - shared, n)
+    def _(j):
+        load(j).start()
+
     pl.semaphore_wait(barrier, rows + cols - 2)
 
     def send_own(j):
@@ -160,10 +203,11 @@
 
     for j in range(AHEAD):
         send_own(j)
-    acts_load.wait()
     for d in range(1, cols // 2):
-        acts_copy(d).start()
-    sib_copy(0).start()
+        for copy in acts_copies(d):
+            copy.start()
+    for copy in sib_copies(0):
+        copy.start()
 
     def exchange(j):
         own_x(j).wait_recv()
@@ -176,8 +220,13 @@
             send_own(j + AHEAD)
 
     def weigh(j):
+        @pl.loop(j * WEIGHINGS, (j + 1) * WEIGHINGS)
+        def _(k):
+            weigh_rows(k)
+
+    def weigh_rows(j):
         w_copy(j).wait()
-        s = lax.rem(j, 2)
+        s = lax.rem(j, W_RING)
         wide = 1024
 
         @pl.loop(0, wbuf.shape[2] // wide)
@@ -185,9 +234,9 @@
             x = wbuf[s, :, pl.ds(pl.multiple_of(k * wide, wide), wide)].astype(jnp.float32)
             wacc[...] += sublane_sum(x * x)
 
-        @pl.when(j + 2 < n)
+        @pl.when(j + W_RING < n * WEIGHINGS)
         def _():
-            w_copy(j + 2).start()
+            w_copy(j + W_RING).start()
 
     def stats(k):
         for d in range(1, rows):
@@ -199,40 +248,34 @@
         nc_out[k] = factor
         cs_out[k] = lax.rsqrt(factor)
         weight = 1.0 / factor
-        s = lax.rem(k, SLOTS)
-        for b in range(blocks):
-            @pl.loop(0, tall // sub)
-            def _(i):
-                at = pl.ds(pl.multiple_of(i * sub, sub), sub)
-                g = grad[s, b, at, :]
-                to = pl.ds(pl.multiple_of(b * tall + i * sub, sub), sub)
-                sacc[to, :] += lane_sum(g * g * weight)
+        s = slot_of(k)
+
+        for i in range(PIECES * PARTS):
+            g = grad[i][s]
+            sacc[pl.ds(i * thin, thin), :] += lane_sum(g * g * weight)
 
     def compute(k):
         fwd_y(k).wait_recv()
         fwd_x(k).wait_recv()
-        og_store(k).start()
-        s = lax.rem(k, SLOTS)
-
-        @pl.when(k >= SLOTS)
+        s = slot_of(k)
+        @pl.when((k >= FIXED) & (k < n - SLOTS))
         def _():
-            g_store(k - SLOTS).wait()
+            og_store(k).start()
 
         right = og_all.at[k]
         column = jnp.zeros((8, width), jnp.float32)
-        for b in range(blocks):
-            def step(i, column):
-                to = pl.ds(pl.multiple_of(b * tall + i * sub, sub), sub)
-                g = jnp.dot(acts_t[to, :], right[...], preferred_element_type=jnp.float32)
-                grad[s, b, pl.ds(pl.multiple_of(i * sub, sub), sub), :] = g
-                squared = g * g + ADDED_SQUARE
-                rowacc[to, :] += lane_sum(squared)
-                return column + sublane_sum(squared)
-            column = lax.fori_loop(0, tall // sub, step, column)
+        tall = thin * DOT_PARTS
+        for row in range(0, tile_rows, tall):
+            i, low = divmod(row, sub)
+            g = jnp.dot(acts_t[i][low : low + tall, :], right[...], preferred_element_type=jnp.float32)
+            for p in range(DOT_PARTS):
+                grad[row // thin + p][s] = g[p * thin : (p + 1) * thin]
+            squared = g * g + ADDED_SQUARE
+            rowacc[pl.ds(row, tall), :] += lane_sum(squared)
+            column = column + sublane_sum(squared)
         colx[r, k] = jnp.sum(column, axis=0, keepdims=True)
         for d in range(1, rows):
             col_copy(k, d).start()
-        g_store(k).start()
 
         @pl.when(k >= LAG)
         def _():
@@ -247,8 +290,9 @@
         weigh(j)
 
     for d in range(1, cols // 2):
-        acts_copy(d).wait_recv()
-        sib_copy(d).start()
+        for copy, onward in zip(acts_copies(d), sib_copies(d)):
+            copy.wait_recv()
+            onward.start()
 
     @pl.loop(ACTS_FORWARD, ACTS_READY)
     def _(j):
@@ -256,11 +300,8 @@
         weigh(j)
 
     for d in range(cols // 2):
-        sib_copy(d).wait_recv()
-    part = acts_all.shape[1]
-    for q in range(cols):
-        acts_t[:, q * part : (q + 1) * part] = acts_all[q].T
-    acts_store.start()
+        for copy in sib_copies(d):
+            copy.wait_recv()
 
     @pl.loop(ACTS_READY, n)
     def _(j):
@@ -328,19 +369,19 @@
         own_y(j).wait_send()
         fwd_y(j).wait_send()
         fwd_x(j).wait_send()
-        og_store(j).wait()
         for d in range(1, rows):
             col_copy(j, d).wait_send()
 
-    @pl.loop(n - SLOTS, n)
+    @pl.loop(FIXED, n - SLOTS)
     def _(j):
-        g_store(j).wait()
-
-    acts_store.wait()
+        og_store(j).wait()
+
     for d in range(1, cols // 2):
-        acts_copy(d).wait_send()
+        for copy in acts_copies(d):
+            copy.wait_send()
     for d in range(cols // 2):
-        sib_copy(d).wait_send()
+        for copy in sib_copies(d):
+            copy.wait_send()
     for d in range(1, cols):
         row_copy(d).wait_send()
         scb_copy(d).wait_send()
@@ -348,24 +389,111 @@
         scc_copy(d).wait_send()
 
 
-def update_kernel(at_ref, og_ref, w_ref, g_ref, rs_ref, cs_ref, out_ref):
-    i = pl.program_id(1)
-    tall, width = w_ref.shape
-    j = pl.program_id(0)
-    cs = cs_ref[j]
-    kept = tall // KEEP
-    sub = (tall - kept) // DOTS
-
-    def finish(g, at):
-        rs = rs_ref[pl.ds(pl.multiple_of(i * tall + at.start, 16), at.size), :]
-        wide = jnp.concatenate([rs] * (width // 128), axis=1)
-        out_ref[at, :] = (w_ref[at, :].astype(jnp.float32) - g * wide * cs).astype(out_ref.dtype)
-
-    finish(g_ref[0, 0], pl.ds(tall - kept, kept))
-    for k in range(DOTS):
-        left = at_ref[pl.ds(pl.multiple_of(i * tall + k * sub, 16), sub), :]
-        g = jnp.dot(left, og_ref[0], preferred_element_type=jnp.float32)
-        finish(g, pl.ds(k * sub, sub))
+def update_kernel(og_ref, w_ref, rs_ref, cs_ref, *refs):
+    acts_t, refs = refs[:PIECES], refs[PIECES:]
+    grad, refs = refs[: PIECES * PARTS], refs[PIECES * PARTS :]
+    out_ref, og_buf, made_buf, kept_buf, og_sem, in_sem, out_sem = refs
+    n, _, width = og_ref.shape
+    sub = acts_t[0].shape[0]
+    thin = sub // PARTS
+    narrow = width // SPLIT
+    chunks = n - KEPT
+
+    def og_load(t):
+        return pltpu.make_async_copy(og_ref.at[FIXED + t], og_buf.at[lax.rem(t, OG_RING)], og_sem.at[lax.rem(t, OG_RING)])
+
+    def copies(t, out):
+        b = lax.rem(t, RING)
+        made = pl.ds(pl.multiple_of((FIXED + t) * width, width), width)
+        kept = pl.ds(pl.multiple_of(chunk_in(lax.div(t, SPLIT), n) * width + lax.rem(t, SPLIT) * narrow, narrow), narrow)
+        if out:
+            return (pltpu.make_async_copy(made_buf.at[b], out_ref.at[:, made], out_sem.at[0, b]),
+                    pltpu.make_async_copy(kept_buf.at[b], out_ref.at[:, kept], out_sem.at[1, b]))
+        return (pltpu.make_async_copy(w_ref.at[:, made], made_buf.at[b], in_sem.at[0, b]),
+                pltpu.make_async_copy(w_ref.at[:, kept], kept_buf.at[b], in_sem.at[1, b]))
+
+    def finish(g, w, row, cs):
+        rs = rs_ref[pl.ds(row, g.shape[0]), :]
+        wide = jnp.concatenate([rs] * (g.shape[1] // 128), axis=1)
+        return (w.astype(jnp.float32) - g * wide * cs).astype(w.dtype)
+
+    mixed = KEPT * SPLIT
+
+    def each(t, out, act):
+        made, kept = copies(t, out)
+        act(made)
+
+        @pl.when(t < mixed)
+        def _():
+            act(kept)
+
+    def start(copy):
+        copy.start()
+
+    def wait(copy):
+        copy.wait()
+
+    for t in range(LOADS):
+        og_load(t).start()
+        each(t, False, start)
+
+    def body(t, mix):
+        b = lax.rem(t, RING)
+
+        @pl.when(t >= RING - LOADS)
+        def _():
+            each(t - (RING - LOADS), True, wait)
+
+        @pl.when(t + LOADS < chunks)
+        def _():
+            og_load(t + LOADS).start()
+            each(t + LOADS, False, start)
+
+        og_load(t).wait()
+        each(t, False, wait)
+        right = og_buf.at[lax.rem(t, OG_RING)]
+        s = lax.div(t, SPLIT)
+        lanes = pl.ds(pl.multiple_of(lax.rem(t, SPLIT) * narrow, narrow), narrow)
+        made_cs = cs_ref[FIXED + t]
+        kept_cs = cs_ref[chunk_in(s, n), :, lanes] if mix else None
+
+        def make(row):
+            i, low = row // sub, row % sub
+            left = acts_t[i][low : low + ROWS, :]
+            return row, jnp.dot(left, right[...], preferred_element_type=jnp.float32)
+
+        def settle(row, g):
+            at = pl.ds(row, ROWS)
+            made_buf[b, at, :] = finish(g, made_buf[b, at, :], row, made_cs)
+
+        def keep(p):
+            at = pl.ds(p * thin, thin)
+            kept_buf[b, at, :] = finish(grad[p][s, :, lanes], kept_buf[b, at, :], p * thin, kept_cs)
+
+        blocks = sub * PIECES // ROWS
+        parts = PIECES * PARTS
+        last = None
+        for k in range(blocks):
+            g = make(k * ROWS)
+            for p in range(k * parts // blocks, (k + 1) * parts // blocks) if mix else ():
+                keep(p)
+            if last is not None:
+                settle(*last)
+            last = g
+        settle(*last)
+        each(t, True, start)
+
+    @pl.loop(0, mixed)
+    def _(t):
+        body(t, True)
+
+    @pl.loop(mixed, chunks)
+    def _(t):
+        body(t, False)
+
+    @pl.loop(chunks - (RING - LOADS), chunks)
+    def _(t):
+        each(t, True, wait)
 
 
 def with_kernels(rows, cols, activations, output_grads, weight, row_moment, col_moment):
@@ -373,66 +501,60 @@
     part = activations.shape[0]
     tokens = part * cols
     n, width = tile_cols // WIDTH, WIDTH
-    blocks = BLOCKS
-    tall = tile_rows // blocks
-    kept = tall // KEEP
     f32, bf16 = jnp.float32, jnp.bfloat16
     any_space = pl.BlockSpec(memory_space=pl.ANY)
     vmem = pl.BlockSpec(memory_space=pltpu.VMEM)
     dma = pltpu.SemaphoreType.DMA
     flops = 2 * tile_rows * tile_cols * tokens
-    og_all, acts_t, grads, new_row, new_col, rs, cs = pl.pallas_call(
+    sub = tile_rows // PIECES
+    activations, output_grads, weight = (
+        pltpu.with_memory_space_constraint(x, pltpu.HBM) for x in (activations, output_grads, weight))
+    og_all, new_row, new_col, *inner = pl.pallas_call(
         functools.partial(gather_kernel, rows, cols),
         out_shape=(
-            jax.ShapeDtypeStruct((n, tokens, width), bf16),
-            jax.ShapeDtypeStruct((tile_rows, tokens), bf16),
-            jax.ShapeDtypeStruct((n, blocks, kept, width), f32),
+            pltpu.HBM((n, tokens, width), bf16),
             jax.ShapeDtypeStruct((1, tile_rows), f32),
             jax.ShapeDtypeStruct((n, 1, width), f32),
             jax.ShapeDtypeStruct((tile_rows, 128), f32),
             jax.ShapeDtypeStruct((n, 1, width), f32),
+            *([jax.ShapeDtypeStruct((sub, tokens), bf16)] * PIECES),
+            *([jax.ShapeDtypeStruct((KEPT, sub // PARTS, width), f32)] * (PIECES * PARTS)),
         ),
         in_specs=[any_space, any_space, any_space, vmem, vmem],
-        out_specs=(any_space, any_space, any_space, vmem, vmem, vmem, vmem),
+        out_specs=(any_space,) + (vmem,) * (4 + PIECES + PIECES * PARTS),
         scratch_shapes=[
             pltpu.VMEM((n, tokens, width), bf16),
-            pltpu.VMEM((cols, part, tile_rows), bf16),
-            pltpu.VMEM((tile_rows, tokens), bf16),
-            pltpu.VMEM((SLOTS, blocks, tall, width), f32),
-            pltpu.VMEM((2, tile_rows // n, tile_cols), bf16),
-            pltpu.VMEM((tile_rows, 128), f32),
+            pltpu.VMEM((W_RING, tile_rows // (n * WEIGHINGS), tile_cols), bf16),
             pltpu.VMEM((tile_rows, 128), f32),
             pltpu.VMEM((8, 1024), f32),
             pltpu.VMEM((rows, n, 1, width), f32),
             pltpu.VMEM((cols, 1, tile_rows), f32),
             pltpu.VMEM((cols, 2, 128), f32),
             pltpu.VMEM((rows, 3, 128), f32),
-            dma((n,)), dma((2, 4, n)), dma((2, cols // 2)), dma((2, cols // 2)), dma((2, rows, n)),
-            dma((2, cols)), dma((2, cols)), dma((2, rows)), dma((2,)), dma((n,)), dma((SLOTS,)), dma((2,)),
+            dma((n,)), dma((2, 4, n)), dma((2, cols // 2, PIECES)), dma((2, cols // 2, PIECES)), dma((2, rows, n)),
+            dma((2, cols)), dma((2, cols)), dma((2, rows)), dma((W_RING,)), dma((-(-tile_rows // width),)), dma((n,)),
         ],
         compiler_params=pltpu.CompilerParams(
-            collective_id=0, has_side_effects=True, vmem_limit_bytes=62 * 1024 * 1024),
+            collective_id=0, has_side_effects=True, vmem_limit_bytes=GATHER_VMEM),
         cost_estimate=pl.CostEstimate(flops=flops, bytes_accessed=2 * weight.size, transcendentals=0),
         name="gather_stats",
     )(activations, output_grads, weight, row_moment.reshape(1, tile_rows), col_moment.reshape(n, 1, width))
+    og_all = pltpu.with_memory_space_constraint(og_all, pltpu.HBM)
     new_weight = pl.pallas_call(
         update_kernel,
-        grid=(n, blocks),
         out_shape=jax.ShapeDtypeStruct((tile_rows, tile_cols), bf16),
-        in_specs=[
-            pl.BlockSpec((tile_rows, tokens), lambda j, i: (0, 0)),
-            pl.BlockSpec((1, tokens, width), lambda j, i: (j, 0, 0)),
-            pl.BlockSpec((tall, width), lambda j, i: (i, j)),
-            pl.BlockSpec((1, 1, kept, width), lambda j, i: (j, i, 0, 0)),
-            vmem,
-            vmem,
+        in_specs=[any_space, any_space] + [vmem] * len(inner),
+        out_specs=any_space,
+        scratch_shapes=[
+            pltpu.VMEM((OG_RING, tokens, width), bf16),
+            pltpu.VMEM((RING, tile_rows, width), bf16),
+            pltpu.VMEM((RING, tile_rows, width // SPLIT), bf16),
+            dma((OG_RING,)), dma((2, RING)), dma((2, RING)),
         ],
-        out_specs=pl.BlockSpec((tall, width), lambda j, i: (i, j)),
-        compiler_params=pltpu.CompilerParams(
-            dimension_semantics=("arbitrary", "arbitrary"), vmem_limit_bytes=48 * 1024 * 1024),
+        compiler_params=pltpu.CompilerParams(vmem_limit_bytes=UPDATE_VMEM),
         cost_estimate=pl.CostEstimate(flops=flops, bytes_accessed=4 * weight.size, transcendentals=0),
         name="update_weight",
-    )(acts_t, og_all, weight, grads, rs, cs)
+    )(og_all, weight, *inner)
     return new_weight, new_row.reshape(tile_rows), new_col.reshape(tile_cols)
 
 
@@ -478,8 +600,9 @@
     chunks = tile_cols // WIDTH
     fits = (
         rows == 4 and cols % 2 == 0 and cols > 2
-        and tile_rows % (64 * BLOCKS * KEEP * DOTS) == 0 and tile_rows % (16 * BLOCKS * PIECES) == 0 and tile_cols % 1024 == 0
-        and chunks > ACTS_READY + SLOTS and tile_rows % (16 * chunks) == 0
+        and tile_rows % (64 * PIECES * PARTS) == 0 and tile_rows % (PIECES * ROWS) == 0 and tile_cols % 1024 == 0
+        and chunks > max(ACTS_READY, KEPT) + SLOTS and tile_rows % (8 * chunks * WEIGHINGS) == 0
+        and chunks >= KEPT * (SPLIT + 1) and tile_rows % ROWS == 0 and 2 * activations.shape[0] <= output_grads.shape[0]
         and output_grads.shape[0] % 32 == 0 and activations.shape[0] % 128 == 0
     )
     args = (activations, output_grads, weight, row_moment, col_moment)

time: 255 us -> 234 us (0.918)
  Pallas kernels: 247 us -> 230 us
  local copies, waits for them, and re-layouts: 6.31 us -> 2.1 us
    pallas_call x2, Pallas kernels: 247 us -> 230 us  [the longest x1 183 us: with_kernels(): pl.pallas_call(functools.partial(gather_kernel, rows, cols), out_shape=(p...]
    unnamed x11 -> x3, local copies, waits for them, and re-layouts: 4.99 us -> 1.38 us
where the time goes in v1:
time: 234 us
  Pallas kernels  230 us (98%)
    pallas_call x1, Pallas kernels, with_kernels(): pl.pallas_call(functools.partial(gather_kernel, rows, cols), out_shape=(p...  183 us
    pallas_call x1, Pallas kernels, with_kernels(): pl.pallas_call(update_kernel, out_shape=jax.ShapeDtypeStruct((tile_rows,...  47 us

profile of v1, /device:TPU:0, one launch (start us, length us, event | category | flops | bytes accessed | tf_op | source)
XLA Modules:
  0.0 233.7 jit_solution(16475851187809117700)
XLA Ops:
  0.6 0.7 reshape.18.rm_ref
  1.3 0.0 copy-start
  1.3 0.8 copy-done
  2.1 183.3 %gather_stats.1 = (bf16[18,1024,512]{2,1,0:T(8,128)(2,1)}, f32[1,2304]{1,0:T(1,128)S(1)}, f32[18,1,512]{2,1,0:T(1,128)S(1)}, f32[2304,128]{1,0:T(8,128)S(1)}, f3...) custom-call(bf16[128,2304]{1,0:T(8,128)(2,1)} %acts_ref.1, ...), custom_call_target="tpu_custom_call" | custom-call | flops 43486543872 | bytes 42467328 | tf_op jit(solution)/shard_map/gather_stats/pallas_call | solution.py:512
  185.4 47.0 %update_weight.1 = bf16[2304,9216]{1,0:T(8,128)(2,1)} custom-call(bf16[18,1024,512]{2,1,0:T(8,128)(2,1)} %get-tuple-element.23.og_ref, bf16[2304,9216]{1,0:T(8,128)(2,1)} %w_ref.3, f32[2304,128]{1,0:T(8,128)S(1)} %get-tuple-element.24.rs_ref, f32[18,1,512]{2,1,0:T(1,128)S(1)} %get-tuple-element.25.cs_ref, bf16[768,1024]{1,0:T(8,128)(2,1)S(1)} %get-tuple-element.26.refs_0_, ...), custom_call_target="tpu_custom_call" | custom-call | flops 43486543872 | bytes 84934656 | tf_op jit(solution)/shard_map/update_weight/pallas_call | solution.py:543
  232.4 0.6 reduce
  233.1 0.6 copy.9
Async XLA Ops:
  1.3 0.8 copy-start

commit v2 on v1

--- a/solution.py
+++ b/solution.py
@@ -287,7 +287,8 @@
     @pl.loop(0, ACTS_FORWARD)
     def _(j):
         exchange(j)
-        weigh(j)
+        weigh(2 * j)
+        weigh(2 * j + 1)
 
     for d in range(1, cols // 2):
         for copy, onward in zip(acts_copies(d), sib_copies(d)):
@@ -297,7 +298,8 @@
     @pl.loop(ACTS_FORWARD, ACTS_READY)
     def _(j):
         exchange(j)
-        weigh(j)
+        weigh(2 * j)
+        weigh(2 * j + 1)
 
     for d in range(cols // 2):
         for copy in sib_copies(d):
@@ -306,7 +308,10 @@
     @pl.loop(ACTS_READY, n)
     def _(j):
         exchange(j)
-        weigh(j)
+
+        @pl.when(j >= 2 * ACTS_READY)
+        def _():
+            weigh(j)
 
         @pl.loop(reach(j - 1), reach(j))
         def _(k):
@@ -601,7 +606,7 @@
     fits = (
         rows == 4 and cols % 2 == 0 and cols > 2
         and tile_rows % (64 * PIECES * PARTS) == 0 and tile_rows % (PIECES * ROWS) == 0 and tile_cols % 1024 == 0
-        and chunks > max(ACTS_READY, KEPT) + SLOTS and tile_rows % (8 * chunks * WEIGHINGS) == 0
+        and chunks > max(2 * ACTS_READY, KEPT + SLOTS) and tile_rows % (8 * chunks * WEIGHINGS) == 0
         and chunks >= KEPT * (SPLIT + 1) and tile_rows % ROWS == 0 and 2 * activations.shape[0] <= output_grads.shape[0]
         and output_grads.shape[0] % 32 == 0 and activations.shape[0] % 128 == 0
     )

time: 234 us -> 234 us (level)
  no operation moved by 1% of the time
where the time goes in v2:
time: 234 us
  Pallas kernels  230 us (98%)
    pallas_call x1, Pallas kernels, with_kernels(): pl.pallas_call(functools.partial(gather_kernel, rows, cols), out_shape=(p...  183 us
    pallas_call x1, Pallas kernels, with_kernels(): pl.pallas_call(update_kernel, out_shape=jax.ShapeDtypeStruct((tile_rows,...  47 us

profile of v2, /device:TPU:0, one launch (start us, length us, event | category | flops | bytes accessed | tf_op | source)
XLA Modules:
  0.0 233.7 jit_solution(18152469550055830915)
XLA Ops:
  0.6 0.7 reshape.18.rm_ref
  1.3 0.0 copy-start
  1.3 0.8 copy-done
  2.1 183.3 %gather_stats.1 = (bf16[18,1024,512]{2,1,0:T(8,128)(2,1)}, f32[1,2304]{1,0:T(1,128)S(1)}, f32[18,1,512]{2,1,0:T(1,128)S(1)}, f32[2304,128]{1,0:T(8,128)S(1)}, f3...) custom-call(bf16[128,2304]{1,0:T(8,128)(2,1)} %acts_ref.1, ...), custom_call_target="tpu_custom_call" | custom-call | flops 43486543872 | bytes 42467328 | tf_op jit(solution)/shard_map/gather_stats/pallas_call | solution.py:517
  185.4 47.0 %update_weight.1 = bf16[2304,9216]{1,0:T(8,128)(2,1)} custom-call(bf16[18,1024,512]{2,1,0:T(8,128)(2,1)} %get-tuple-element.23.og_ref, bf16[2304,9216]{1,0:T(8,128)(2,1)} %w_ref.3, f32[2304,128]{1,0:T(8,128)S(1)} %get-tuple-element.24.rs_ref, f32[18,1,512]{2,1,0:T(1,128)S(1)} %get-tuple-element.25.cs_ref, bf16[768,1024]{1,0:T(8,128)(2,1)S(1)} %get-tuple-element.26.refs_0_, ...), custom_call_target="tpu_custom_call" | custom-call | flops 43486543872 | bytes 84934656 | tf_op jit(solution)/shard_map/update_weight/pallas_call | solution.py:548
  232.5 0.6 reduce
  233.1 0.6 copy.9
Async XLA Ops:
  1.3 0.8 copy-start
